TPU v7x, 128 devices: a 2x2x16 block of a 8x8x16 slice. The times are simulated.
128 devices in a mesh: groups: 4 (over y, x), seq: 16 (over z), sub: 2 (over core).
Axes of the slice: x: 2, y: 2, z: 16, core: 2. Of those that a mesh axis runs over, the one named last changes fastest.
The devices are a block of a 8x8x16 slice.
Arguments:
- query_proj: bfloat16 [8192, 4096], P(('groups', 'seq'), 'sub'), parts along dimension 0, may hold values from -2500 to 2500
- key_proj: bfloat16 [8192, 4096], P(('groups', 'seq'), 'sub'), parts along dimension 0, may hold values from -2500 to 2500
- value_proj: bfloat16 [8192, 4096], P(('groups', 'seq'), 'sub'), parts along dimension 0, may hold values from -12 to 12
- out_weight: bfloat16 [4096, 5120], P('sub', 'seq'), may hold values from -0.5 to 0.5
- query_gain: float32 [4096], P('sub'), may hold values from 0.25 to 1.75
- key_gain: float32 [4096], P('sub'), may hold values from 0.25 to 1.75
- gate_scale: float32 [20480], P(('groups', 'sub')), parts along dimension 0, may hold values from 0.5 to 2
- key_count: int32 [4], P('groups'), parts along dimension 0, may hold values from 1024 to 2048
Outputs:
- attended_out: bfloat16 [8192, 5120], P(('groups', 'seq'), 'sub'), parts along dimension 0
There are 4 independent parts, one for each index of `groups`. A program takes and returns all parts, laid end to end along the dimension named above; an argument that names none is the same for every part. Nothing has to cross between parts.
All inputs are finite; a program needn't handle non-finite values.
Results may differ from a plain program's by a relative error of at most 0.012.
Values may be sent and summed in bfloat16 or wider, within the bound.
A program may use at most 128 MiB of HBM per device.

v0:
```python
import math
import jax
import jax.numpy as jnp
from jax import lax
from jax.sharding import PartitionSpec as P

HD = 128
epsilon = 1e-06
key_block = 512


def gathered_total(array, axis):
    return lax.all_gather(array, axis).sum(0)


def cut_along(array, dim, size):
    shape = array.shape
    pieces = array.reshape(*shape[:dim], size, shape[dim] // size, *shape[dim + 1 :])
    return jnp.moveaxis(pieces, dim, 0)


def sent_and_summed(array, axis, dim):
    pieces = cut_along(array, dim, lax.axis_size(axis))
    arrived = lax.all_to_all(pieces, axis, split_axis=0, concat_axis=0, tiled=True)
    return arrived.astype(jnp.float32).sum(axis=0)


def fold_keys(running, queries, key_rows, value_rows, offset, live_keys):
    row_total = key_rows.shape[0]
    blocks = row_total // key_block
    head_count = queries.shape[1]
    key_blocks = key_rows.reshape(blocks, key_block, head_count, HD)
    value_blocks = value_rows.reshape(blocks, key_block, head_count, HD)
    scale = 1.0 / math.sqrt(HD)

    def one_block(running, element):
        key_piece, value_piece, block_index = element
        highest, weight_sum, accumulated = running
        scores = (
            jnp.einsum("qhd,khd->hqk", queries, key_piece, preferred_element_type=jnp.float32)
            * scale
        )
        positions = offset + block_index * key_block + jnp.arange(key_block)
        usable = (positions < live_keys)[None, None, :]
        scores = jnp.where(usable, scores, -1e30)
        newest = jnp.maximum(highest, jnp.max(scores, axis=2))
        shrink = jnp.exp(highest - newest)
        weights = jnp.where(usable, jnp.exp(scores - newest[:, :, None]), 0.0)
        weight_sum = weight_sum * shrink + jnp.sum(weights, axis=2)
        product = jnp.einsum(
            "hqk,khd->qhd",
            weights.astype(jnp.bfloat16),
            value_piece,
            preferred_element_type=jnp.float32,
        )
        accumulated = accumulated * shrink.T[:, :, None] + product
        return ((newest, weight_sum, accumulated), None)

    running, unused = lax.scan(one_block, running, (key_blocks, value_blocks, jnp.arange(blocks)))
    return running


def empty_state(query_rows, head_count):
    return (
        jnp.full((head_count, query_rows), -1e30, jnp.float32),
        jnp.zeros((head_count, query_rows), jnp.float32),
        jnp.zeros((query_rows, head_count, HD), jnp.float32),
    )


def finish(running):
    highest, weight_sum, accumulated = running
    result = accumulated / weight_sum.T[:, :, None]
    return result.reshape(result.shape[0], -1).astype(jnp.bfloat16)


def shards(
    query_proj, key_proj, value_proj, out_weight, query_gain, key_gain, gate_scale, key_count
):
    features = query_proj.shape[1]
    query_wide = query_proj.astype(jnp.float32)
    key_wide = key_proj.astype(jnp.float32)
    squares = (
        gathered_total(jnp.sum(query_wide * query_wide, axis=1), "sub"),
        gathered_total(jnp.sum(key_wide * key_wide, axis=1), "sub"),
    )
    all_features = features * lax.axis_size("sub")
    query_normed = (
        query_wide * lax.rsqrt(squares[0] / all_features + epsilon)[:, None] * query_gain
    ).astype(jnp.bfloat16)
    key_normed = (
        key_wide * lax.rsqrt(squares[1] / all_features + epsilon)[:, None] * key_gain
    ).astype(jnp.bfloat16)
    live_keys = key_count[0]
    query_all, key_all, value_all = (
        lax.all_to_all(query_normed, "seq", split_axis=1, concat_axis=0, tiled=True),
        lax.all_to_all(key_normed, "seq", split_axis=1, concat_axis=0, tiled=True),
        lax.all_to_all(value_proj, "seq", split_axis=1, concat_axis=0, tiled=True),
    )
    seq_rows = query_all.shape[0]
    head_count = query_all.shape[1] // HD
    running = fold_keys(
        empty_state(seq_rows, head_count),
        query_all.reshape(seq_rows, head_count, HD),
        key_all,
        value_all,
        0,
        live_keys,
    )
    attended = lax.all_to_all(finish(running), "seq", split_axis=0, concat_axis=1, tiled=True)
    partial_value = jnp.dot(
        attended,
        lax.all_gather(out_weight, "seq", axis=1, tiled=True),
        preferred_element_type=jnp.float32,
    )
    summed = sent_and_summed(partial_value.astype(jnp.bfloat16), "sub", 1)
    return (summed * gate_scale).astype(jnp.bfloat16)


def solution(mesh):
    placed = (
        P(("groups", "seq"), "sub"),
        P(("groups", "seq"), "sub"),
        P(("groups", "seq"), "sub"),
        P("sub", "seq"),
        P("sub"),
        P("sub"),
        P(("groups", "sub")),
        P("groups"),
    )
    return jax.shard_map(
        shards, mesh=mesh, in_specs=placed, out_specs=P(("groups", "seq"), "sub"), check_vma=False
    )
```

profile of v0, /device:TPU:69, one launch (start us, length us, event | category | flops | bytes accessed | tf_op | source)
XLA Modules:
  0.0 359.0 jit_solution(15972077560654113518)
XLA Ops:
  6.5 0.0 copy-start.1
  6.5 0.0 copy-start.4
  6.6 0.0 copy-start.2
  6.6 0.0 all-gather.6.cloned.1.call-start
  6.6 0.7 all-gather.6.cloned.1.call-update
  7.3 1.3 copy.24
  8.6 0.3 fusion.23
  8.9 11.4 %all-gather.2 = f32[2,1,128]{2,1,0:T(1,128)S(1)} all-gather(f32[1,1,128]{2,1,0:T(1,128)S(1)} %bitcast.88), channel_id=2, replica_groups=mesh['groups'=4,'seq'=16,'sub'=2] {'sub'}, dimensions={0}, use_global_device_ids=true | all-gather | bytes 1536 | tf_op jit(solution)/shard_map/all_gather | solution.py:13
  20.4 1.8 fusion.25
  22.2 8.3 %all-to-all-start = ((bf16[128,16,128]{0,2,1:T(8,128)(2,1)}), bf16[128,16,128]{0,2,1:T(8,128)(2,1)S(1)}, u32[]{:S(2)}, u32[]{:S(2)}) async-start(bf16[128,16,128]{0,2,1:T(8,128)(2,1)} %bitcast.2), calls=%async_computation | async-start | bytes 1048576 | tf_op jit(solution)/shard_map/all_to_all | solution.py:97
  30.5 0.0 copy-done.1
  30.5 0.3 copy.26
  30.8 0.3 fusion.26
  31.0 2.1 all-gather.3
  33.2 0.0 copy-done.4
  33.2 1.1 fusion.28
  34.4 26.8 %all-to-all-done = bf16[128,16,128]{0,2,1:T(8,128)(2,1)S(1)} async-done(((bf16[128,16,128]{0,2,1:T(8,128)(2,1)}), bf16[128,16,128]{0,2,1:T(8,128)(2,1)S(1)}, u32[]{:S(2)}, u32[]{:S(2)}) %all-to-all-start) | async-done | bytes 524320 | tf_op jit(solution)/shard_map/all_to_all | solution.py:97
  61.1 10.6 %all-to-all-start.1 = ((bf16[128,16,128]{0,2,1:T(8,128)(2,1)}), bf16[128,16,128]{0,2,1:T(8,128)(2,1)S(1)}, u32[]{:S(2)}, u32[]{:S(2)}) async-start(bf16[128,16,128]{0,2,1:T(8,128)(2,1)} %bitcast.7), calls=%async_computation.1 | async-start | bytes 1048576 | tf_op jit(solution)/shard_map/all_to_all | solution.py:96
  71.7 0.0 copy-done.2
  71.7 1.0 copy.28
  72.7 29.4 %all-to-all-done.1 = bf16[128,16,128]{0,2,1:T(8,128)(2,1)S(1)} async-done(((bf16[128,16,128]{0,2,1:T(8,128)(2,1)}), bf16[128,16,128]{0,2,1:T(8,128)(2,1)S(1)}, u32[]{:S(2)}, u32[]{:S(2)}) %all-to-all-start.1) | async-done | bytes 524320 | tf_op jit(solution)/shard_map/all_to_all | solution.py:96
  102.1 10.9 %all-to-all-start.2 = ((bf16[128,16,128]{0,2,1:T(8,128)(2,1)}), bf16[128,16,128]{0,2,1:T(8,128)(2,1)S(1)}, u32[]{:S(2)}, u32[]{:S(2)}) async-start(bf16[128,16,128]{0,2,1:T(8,128)(2,1)} %bitcast.10), calls=%async_computation.2 | async-start | bytes 1048576 | tf_op jit(solution)/shard_map/all_to_all | solution.py:98
  113.1 0.3 copy.25
  113.4 0.3 copy.27
  113.7 29.6 %all-to-all-done.2 = bf16[128,16,128]{0,2,1:T(8,128)(2,1)S(1)} async-done(((bf16[128,16,128]{0,2,1:T(8,128)(2,1)}), bf16[128,16,128]{0,2,1:T(8,128)(2,1)S(1)}, u32[]{:S(2)}, u32[]{:S(2)}) %all-to-all-start.2) | async-done | bytes 524320 | tf_op jit(solution)/shard_map/all_to_all | solution.py:98
  143.2 1.0 copy.29
  144.3 42.3 %while.15 = (s32[]{:T(128)}, f32[1,2048]{1,0:T(1,128)S(1)}, f32[1,2048]{1,0:T(1,128)S(1)}, f32[2048,1,128]{0,2,1:T(8,128)S(1)}, s32[4]{0:T(128)S(1)}, /*index=5*...) while((s32[]{:T(128)}, f32[1,2048]{1,0:T(1,128)S(1)}, ...), condition=%wide.region_7.8_spmd.clone, body=%wide.region_4.7_spmd.clone.sunk | while | flops 551300096 | bytes 32377536 | solution.py:59
  144.3 0.6 dynamic_slice.29
  145.5 0.7 add_compare_fusion.2
  146.2 2.7 fusion.40
  148.9 0.0 copy-start
  148.9 3.6 %fusion.42 = f32[2048]{0:T(1024)S(1)} fusion(f32[512,2048]{1,0:T(8,128)} %get-tuple-element.194, f32[2048]{0:T(1024)S(1)} %bitcast.74, pred[512]{0:T(512)(128)(4,1)S(1)} %add_compare_fusion.2), kind=kLoop, calls=%fused_computation.3.clone.1 | loop fusion | flops 5240832 | bytes 4211200 | tf_op jit(solution)/shard_map/while/body/eval_jaxpr/reduce_sum | solution.py:49
  152.6 0.0 copy-done
  152.6 2.2 fusion.44
  154.8 0.6 dynamic_slice.29
  156.1 0.7 add_compare_fusion.2
  156.7 2.7 fusion.40
  159.5 3.6 %fusion.42 = f32[2048]{0:T(1024)S(1)} fusion(f32[512,2048]{1,0:T(8,128)} %get-tuple-element.194, f32[2048]{0:T(1024)S(1)} %bitcast.74, pred[512]{0:T(512)(128)(4,1)S(1)} %add_compare_fusion.2), kind=kLoop, calls=%fused_computation.3.clone.1 | loop fusion | flops 5240832 | bytes 4211200 | tf_op jit(solution)/shard_map/while/body/eval_jaxpr/reduce_sum | solution.py:49
  163.1 0.0 copy-done
  163.1 2.2 fusion.44
  165.4 0.6 dynamic_slice.29
  166.6 0.7 add_compare_fusion.2
  167.3 2.7 fusion.40
  170.0 3.6 %fusion.42 = f32[2048]{0:T(1024)S(1)} fusion(f32[512,2048]{1,0:T(8,128)} %get-tuple-element.194, f32[2048]{0:T(1024)S(1)} %bitcast.74, pred[512]{0:T(512)(128)(4,1)S(1)} %add_compare_fusion.2), kind=kLoop, calls=%fused_computation.3.clone.1 | loop fusion | flops 5240832 | bytes 4211200 | tf_op jit(solution)/shard_map/while/body/eval_jaxpr/reduce_sum | solution.py:49
  173.7 0.0 copy-done
  173.7 2.2 fusion.44
  176.0 0.6 dynamic_slice.29
  177.2 0.7 add_compare_fusion.2
  177.9 2.7 fusion.40
  180.6 3.6 %fusion.42 = f32[2048]{0:T(1024)S(1)} fusion(f32[512,2048]{1,0:T(8,128)} %get-tuple-element.194, f32[2048]{0:T(1024)S(1)} %bitcast.74, pred[512]{0:T(512)(128)(4,1)S(1)} %add_compare_fusion.2), kind=kLoop, calls=%fused_computation.3.clone.1 | loop fusion | flops 5240832 | bytes 4211200 | tf_op jit(solution)/shard_map/while/body/eval_jaxpr/reduce_sum | solution.py:49
  184.3 0.0 copy-done
  184.3 2.2 fusion.44
  186.6 0.3 copy.32
  186.9 0.3 divide_convert_fusion
  187.2 41.0 %all_to_all.69 = bf16[16,128,128]{2,1,0:T(8,128)(2,1)S(1)} all-to-all(bf16[16,128,128]{2,1,0:T(8,128)(2,1)S(1)} %bitcast.78), channel_id=1, replica_groups=mesh['groups'=4,'seq'=16,'sub'=2] {'seq'}, dimensions={0} | all-to-all | bytes 1048576 | tf_op jit(solution)/shard_map/all_to_all | solution.py:110
  228.3 0.3 copy.33
  228.5 105.7 %all-gather.6.cloned.1.call-done = bf16[2048,5120]{0,1:T(8,128)(2,1)} async-done(((bf16[2048,320]{0,1:T(8,128)(2,1)}), bf16[2048,5120]{0,1:T(8,128)(2,1)}) %all-gather.6.cloned.1.call-update) | async-done | bytes 20971536 | tf_op jit(solution)/shard_map/all_gather | solution.py:113
  334.3 11.4 %convolution_convert_fusion = bf16[128,5120]{1,0:T(8,128)(2,1)S(1)} fusion(bf16[128,2048]{0,1:T(8,128)(2,1)S(1)} %bitcast.76, bf16[2048,5120]{0,1:T(8,128)(2,1)} %all-gather.6.cloned.1.call-done), kind=kOutput, calls=%fused_computation.30 | convolution fusion | flops 2685009920 | bytes 22806528 | tf_op jit(solution)/shard_map/dot_general | solution.py:111
  345.7 0.0 copy-start.3
  345.7 0.1 copy.37
  345.8 5.3 %all_to_all.70 = bf16[2,128,2560]{2,1,0:T(8,128)(2,1)S(1)} all-to-all(bf16[2,128,2560]{2,1,0:T(8,128)(2,1)S(1)} %bitcast.72), channel_id=1, replica_groups=mesh['groups'=4,'seq'=16,'sub'=2] {'sub'}, dimensions={0} | all-to-all | bytes 2621440 | tf_op jit(solution)/shard_map/all_to_all | solution.py:24
  351.1 0.2 convert_reduce_fusion
  351.3 0.0 copy-done.3
  351.3 0.9 multiply_convert_fusion
  (23 shorter events, 0.3 us)
Async XLA Ops:
  6.5 23.9 %copy-start.1 = (bf16[128,2048]{1,0:T(8,128)(2,1)S(1)}, bf16[128,2048]{1,0:T(8,128)(2,1)}, u32[]{:S(2)}) copy-start(bf16[128,2048]{1,0:T(8,128)(2,1)} %param.10) | copy-start | bytes 1572868
  6.5 26.7 %copy-start.4 = (f32[2048]{0:T(1024)S(1)}, f32[2048]{0:T(1024)}, u32[]{:S(2)}) copy-start(f32[2048]{0:T(1024)} %param.14) | copy-start | bytes 24580
  6.6 65.2 %copy-start.2 = (bf16[128,2048]{1,0:T(8,128)(2,1)S(1)}, bf16[128,2048]{1,0:T(8,128)(2,1)}, u32[]{:S(2)}) copy-start(bf16[128,2048]{1,0:T(8,128)(2,1)} %param.12) | copy-start | bytes 1572868
  6.6 327.7 %all-gather.6.cloned.1.call-start = ((), (), s32[]{:S(2)}) async-start(), calls=%async_computation.5 | async-start | bytes 22282240 | tf_op jit(solution)/shard_map/all_gather | solution.py:113
  22.2 39.0 %all-to-all-start = ((bf16[128,16,128]{0,2,1:T(8,128)(2,1)}), bf16[128,16,128]{0,2,1:T(8,128)(2,1)S(1)}, u32[]{:S(2)}, u32[]{:S(2)}) async-start(bf16[128,16,128]{0,2,1:T(8,128)(2,1)} %bitcast.2), calls=%async_computation | async-start | bytes 1048576 | tf_op jit(solution)/shard_map/all_to_all | solution.py:97
  61.1 41.0 %all-to-all-start.1 = ((bf16[128,16,128]{0,2,1:T(8,128)(2,1)}), bf16[128,16,128]{0,2,1:T(8,128)(2,1)S(1)}, u32[]{:S(2)}, u32[]{:S(2)}) async-start(bf16[128,16,128]{0,2,1:T(8,128)(2,1)} %bitcast.7), calls=%async_computation.1 | async-start | bytes 1048576 | tf_op jit(solution)/shard_map/all_to_all | solution.py:96
  102.1 41.1 %all-to-all-start.2 = ((bf16[128,16,128]{0,2,1:T(8,128)(2,1)}), bf16[128,16,128]{0,2,1:T(8,128)(2,1)S(1)}, u32[]{:S(2)}, u32[]{:S(2)}) async-start(bf16[128,16,128]{0,2,1:T(8,128)(2,1)} %bitcast.10), calls=%async_computation.2 | async-start | bytes 1048576 | tf_op jit(solution)/shard_map/all_to_all | solution.py:98
  148.9 3.7 %copy-start = (f32[512,2048]{1,0:T(8,128)S(1)}, f32[512,2048]{1,0:T(8,128)}, u32[]{:S(2)}) copy-start(f32[512,2048]{1,0:T(8,128)} %get-tuple-element.194) | copy-start | bytes 12582916 | tf_op jit(solution)/shard_map/while
  159.4 3.7 %copy-start = (f32[512,2048]{1,0:T(8,128)S(1)}, f32[512,2048]{1,0:T(8,128)}, u32[]{:S(2)}) copy-start(f32[512,2048]{1,0:T(8,128)} %get-tuple-element.194) | copy-start | bytes 12582916 | tf_op jit(solution)/shard_map/while
  170.0 3.7 %copy-start = (f32[512,2048]{1,0:T(8,128)S(1)}, f32[512,2048]{1,0:T(8,128)}, u32[]{:S(2)}) copy-start(f32[512,2048]{1,0:T(8,128)} %get-tuple-element.194) | copy-start | bytes 12582916 | tf_op jit(solution)/shard_map/while
  180.6 3.7 %copy-start = (f32[512,2048]{1,0:T(8,128)S(1)}, f32[512,2048]{1,0:T(8,128)}, u32[]{:S(2)}) copy-start(f32[512,2048]{1,0:T(8,128)} %get-tuple-element.194) | copy-start | bytes 12582916 | tf_op jit(solution)/shard_map/while
  345.7 5.6 %copy-start.3 = (f32[2560]{0:T(1024)S(1)}, f32[2560]{0:T(1024)}, u32[]{:S(2)}) copy-start(f32[2560]{0:T(1024)} %param.16) | copy-start | bytes 30724
Sparse Core Ops, SparseCore 0:
  9.0 325.2 all-gather.5
where the time goes:
time: 360 us; the launch traced here: 359 us
  waiting for transfers between devices  192 us (53%)
  blocking collectives  59.8 us (17%)
  matrix products  31.2 us (9%)
  starting transfers between devices  29.8 us (8%)
  other arithmetic  22.4 us (6%)
  between operations  13.6 us (4%)
  local copies, waits for them, and re-layouts  7.39 us (2%)
    all_gather x1, waiting for transfers between devices, shards(): lax.all_gather(out_weight, 'seq', axis=1, tiled=True)  106 us
    all_to_all x1, blocking collectives, shards(): lax.all_to_all(finish(running), 'seq', split_axis=0, concat_axis=1, tiled...  41 us
    all_to_all x1, waiting for transfers between devices, shards(): lax.all_to_all(value_proj, 'seq', split_axis=1, concat_axis=0, tiled=True)  29.6 us
    all_to_all x1, waiting for transfers between devices, shards(): lax.all_to_all(query_normed, 'seq', split_axis=1, concat_axis=0, tiled=True)  29.4 us
    all_to_all x1, waiting for transfers between devices, shards(): lax.all_to_all(key_normed, 'seq', split_axis=1, concat_axis=0, tiled=True)  26.8 us
    reduce_sum x4, other arithmetic, one_block(): weight_sum = weight_sum * shrink + jnp.sum(weights, axis=2)  14.5 us
    all_gather x2, blocking collectives, gathered_total(): return lax.all_gather(array, axis).sum(0)  13.5 us
    dot_general x1, matrix products, shards(): jnp.dot(attended, lax.all_gather(out_weight, 'seq', axis=1, tiled=True),...  11.4 us
  transfers between devices with their start and end apart: 4, of which 4 were waited for; matrix products, arithmetic and copies ran while one was open for 13% of the time, Pallas kernels for 0%

commit v1 on v0

--- a/solution.py
+++ b/solution.py
@@ -7,6 +7,11 @@
 HD = 128
 epsilon = 1e-06
 key_block = 512
+
+
+def gather_over(x, axis, d):
+    sent = jnp.stack([x] * lax.axis_size(axis))
+    return jnp.concatenate(lax.all_to_all(sent, axis, 0, 0), axis=d)
 
 
 def gathered_total(array, axis):
@@ -109,9 +114,7 @@
     )
     attended = lax.all_to_all(finish(running), "seq", split_axis=0, concat_axis=1, tiled=True)
     partial_value = jnp.dot(
-        attended,
-        lax.all_gather(out_weight, "seq", axis=1, tiled=True),
-        preferred_element_type=jnp.float32,
+        attended, gather_over(out_weight, "seq", 1), preferred_element_type=jnp.float32
     )
     summed = sent_and_summed(partial_value.astype(jnp.bfloat16), "sub", 1)
     return (summed * gate_scale).astype(jnp.bfloat16)

time: 360 us -> 1120 us (3.11)
  waiting for transfers between devices: 192 us -> 962 us
  starting transfers between devices: 29.8 us -> 47.1 us
  between operations: 13.6 us -> 0.19 us
  matrix products: 31.2 us -> 19.7 us
    all_to_all x0 -> x1, waiting for transfers between devices: none -> 900 us  [gather_over(): return jnp.concatenate(lax.all_to_all(sent, axis, 0, 0), axis=d)]
    all_gather x1 -> x0, waiting for transfers between devices: 106 us -> none  [shards(): lax.all_gather(out_weight, 'seq', axis=1, tiled=True)]
    all_to_all x0 -> x1, starting transfers between devices: none -> 12.9 us  [gather_over(): return jnp.concatenate(lax.all_to_all(sent, axis, 0, 0), axis=d)]
    all_to_all x1, waiting for transfers between devices: 29.4 us -> 17.6 us  [shards(): lax.all_to_all(query_normed, 'seq', split_axis=1, concat_axis=0, tiled=True)]
  transfers between devices with their start and end apart: 4 -> 4, of which waited for: 4 -> 4; matrix products, arithmetic and copies ran while one was open for 13% -> 0% of each run, Pallas kernels for 0% -> 0%
where the time goes in v1:
time: 1120 us; the launch traced here: 1110 us
  waiting for transfers between devices  962 us (86%)
  blocking collectives  54.8 us (5%)
  starting transfers between devices  47.1 us (4%)
  matrix products  19.7 us (2%)
  local copies, waits for them, and re-layouts  15.3 us (1%)
  other arithmetic  13 us (1%)
    all_to_all x1, waiting for transfers between devices, gather_over(): return jnp.concatenate(lax.all_to_all(sent, axis, 0, 0), axis=d)  900 us
    all_to_all x1, blocking collectives, shards(): lax.all_to_all(finish(running), 'seq', split_axis=0, concat_axis=1, tiled...  35.4 us
  transfers between devices with their start and end apart: 4, of which 4 were waited for; matrix products, arithmetic and copies ran while one was open for 0% of the time, Pallas kernels for 0%

profile of v1, /device:TPU:69, one launch (start us, length us, event | category | flops | bytes accessed | tf_op | source)
XLA Modules:
  0.0 1114.9 jit_solution(8410578874869810362)
XLA Ops:
  0.0 0.0 copy-start.3
  0.0 0.0 copy-start.1
  0.0 1.4 copy.27
  1.4 0.3 fusion.26
  1.7 11.4 %all-gather.3 = f32[2,1,128]{2,1,0:T(1,128)S(1)} all-gather(f32[1,1,128]{2,1,0:T(1,128)S(1)} %bitcast.91), channel_id=3, replica_groups=mesh['groups'=4,'seq'=16,'sub'=2] {'sub'}, dimensions={0}, use_global_device_ids=true | all-gather | bytes 1536 | tf_op jit(solution)/shard_map/all_gather | solution.py:18
  13.1 1.8 fusion.28
  14.9 8.3 all-to-all-start.1
  23.2 1.3 copy.25
  24.5 0.3 fusion.23
  24.8 2.1 all-gather.2
  27.0 0.0 copy-done.3
  27.0 1.1 fusion.25
  28.1 17.6 %all-to-all-done.1 = bf16[128,16,128]{0,2,1:T(8,128)(2,1)S(1)} async-done(((bf16[128,16,128]{0,2,1:T(8,128)(2,1)}), bf16[128,16,128]{0,2,1:T(8,128)(2,1)S(1)}, u32[]{:S(2)}, u32[]{:S(2)}) %all-to-all-start.1) | async-done | bytes 524320 | tf_op jit(solution)/shard_map/all_to_all | solution.py:101
  45.7 13.1 %all-to-all-start = ((bf16[128,16,128]{0,2,1:T(8,128)(2,1)}), bf16[128,16,128]{0,2,1:T(8,128)(2,1)S(1)}, u32[]{:S(2)}, u32[]{:S(2)}) async-start(bf16[128,16,128]{0,2,1:T(8,128)(2,1)} %bitcast.2), calls=%async_computation | async-start | bytes 1048576 | tf_op jit(solution)/shard_map/all_to_all | solution.py:102
  58.8 0.0 copy-done.1
  58.8 1.0 copy.29
  59.8 21.7 %all-to-all-done = bf16[128,16,128]{0,2,1:T(8,128)(2,1)S(1)} async-done(((bf16[128,16,128]{0,2,1:T(8,128)(2,1)}), bf16[128,16,128]{0,2,1:T(8,128)(2,1)S(1)}, u32[]{:S(2)}, u32[]{:S(2)}) %all-to-all-start) | async-done | bytes 524320 | tf_op jit(solution)/shard_map/all_to_all | solution.py:102
  81.5 12.8 %all-to-all-start.2 = ((bf16[128,16,128]{0,2,1:T(8,128)(2,1)}), bf16[128,16,128]{0,2,1:T(8,128)(2,1)S(1)}, u32[]{:S(2)}, u32[]{:S(2)}) async-start(bf16[128,16,128]{0,2,1:T(8,128)(2,1)} %bitcast.10), calls=%async_computation.2 | async-start | bytes 1048576 | tf_op jit(solution)/shard_map/all_to_all | solution.py:103
  94.4 0.3 copy.28
  94.7 0.3 copy.26
  95.0 22.1 %all-to-all-done.2 = bf16[128,16,128]{0,2,1:T(8,128)(2,1)S(1)} async-done(((bf16[128,16,128]{0,2,1:T(8,128)(2,1)}), bf16[128,16,128]{0,2,1:T(8,128)(2,1)S(1)}, u32[]{:S(2)}, u32[]{:S(2)}) %all-to-all-start.2) | async-done | bytes 524320 | tf_op jit(solution)/shard_map/all_to_all | solution.py:103
  117.1 0.3 copy.30
  117.4 22.0 %while.15 = (s32[]{:T(128)}, f32[1,2048]{1,0:T(1,128)S(1)}, f32[1,2048]{1,0:T(1,128)S(1)}, f32[2048,1,128]{0,2,1:T(8,128)S(1)}, s32[4]{0:T(128)S(1)}, /*index=5*...) while((s32[]{:T(128)}, f32[1,2048]{1,0:T(1,128)S(1)}, ...), condition=%wide.region_7.8_spmd.clone, body=%wide.region_4.7_spmd.clone.sunk | while | flops 551300096 | bytes 15599793 | solution.py:64
  117.4 0.7 dynamic_slice.29
  118.8 0.7 add_compare_fusion.2
  119.4 0.8 fusion.40
  120.2 1.3 fusion.42
  121.6 1.3 fusion.44
  122.9 0.7 dynamic_slice.29
  124.3 0.7 add_compare_fusion.2
  124.9 0.8 fusion.40
  125.7 1.3 fusion.42
  127.1 1.3 fusion.44
  128.4 0.7 dynamic_slice.29
  129.8 0.7 add_compare_fusion.2
  130.4 0.8 fusion.40
  131.2 1.3 fusion.42
  132.6 1.3 fusion.44
  133.9 0.7 dynamic_slice.29
  135.3 0.7 add_compare_fusion.2
  135.9 0.8 fusion.40
  136.7 1.3 fusion.42
  138.1 1.3 fusion.44
  139.4 0.0 copy-start
  139.4 0.3 copy.33
  139.8 0.3 divide_convert_fusion
  140.1 35.4 %all_to_all.74 = bf16[16,128,128]{2,1,0:T(8,128)(2,1)S(1)} all-to-all(bf16[16,128,128]{2,1,0:T(8,128)(2,1)S(1)} %bitcast.81), channel_id=1, replica_groups=mesh['groups'=4,'seq'=16,'sub'=2] {'seq'}, dimensions={0} | all-to-all | bytes 1048576 | tf_op jit(solution)/shard_map/all_to_all | solution.py:115
  175.5 0.0 copy-done
  175.5 7.3 stack.2
  182.8 12.9 %all-to-all-start.4 = ((bf16[16,2048,320]{1,2,0:T(8,128)(2,1)}), bf16[16,2048,320]{1,2,0:T(8,128)(2,1)}, u32[]{:S(2)}, u32[]{:S(2)}) async-start(bf16[16,2048,320]{1,2,0:T(8,128)(2,1)} %stack.2), calls=%async_computation.4 | async-start | bytes 41943040 | tf_op jit(solution)/shard_map/all_to_all | solution.py:14
  195.7 0.3 copy.34
  196.0 900.4 %all-to-all-done.4 = bf16[16,2048,320]{1,2,0:T(8,128)(2,1)} async-done(((bf16[16,2048,320]{1,2,0:T(8,128)(2,1)}), bf16[16,2048,320]{1,2,0:T(8,128)(2,1)}, u32[]{:S(2)}, u32[]{:S(2)}) %all-to-all-start.4) | async-done | bytes 20971552 | tf_op jit(solution)/shard_map/all_to_all | solution.py:14
  1096.4 11.4 %convolution_convert_fusion = bf16[128,5120]{1,0:T(8,128)(2,1)S(1)} fusion(bf16[128,2048]{0,1:T(8,128)(2,1)S(1)} %bitcast.79, bf16[2048,5120]{0,1:T(8,128)(2,1)} %bitcast.19), kind=kOutput, calls=%fused_computation.30 | convolution fusion | flops 2685009920 | bytes 22806528 | tf_op jit(solution)/shard_map/dot_general | solution.py:116
  1107.8 0.0 copy-start.2
  1107.8 0.1 copy.38
  1107.9 5.8 all_to_all.75
  1113.8 0.2 convert_reduce_fusion
  1114.0 0.0 copy-done.2
  1114.0 0.9 multiply_convert_fusion
  (20 shorter events, 0.3 us)
Async XLA Ops:
  0.0 27.0 %copy-start.3 = (f32[2048]{0:T(1024)S(1)}, f32[2048]{0:T(1024)}, u32[]{:S(2)}) copy-start(f32[2048]{0:T(1024)} %param.15) | copy-start | bytes 24580
  0.0 58.8 %copy-start.1 = (bf16[128,2048]{1,0:T(8,128)(2,1)S(1)}, bf16[128,2048]{1,0:T(8,128)(2,1)}, u32[]{:S(2)}) copy-start(bf16[128,2048]{1,0:T(8,128)(2,1)} %param.12) | copy-start | bytes 1572868
  14.9 30.8 %all-to-all-start.1 = ((bf16[128,16,128]{0,2,1:T(8,128)(2,1)}), bf16[128,16,128]{0,2,1:T(8,128)(2,1)S(1)}, u32[]{:S(2)}, u32[]{:S(2)}) async-start(bf16[128,16,128]{0,2,1:T(8,128)(2,1)} %bitcast.7), calls=%async_computation.1 | async-start | bytes 1048576 | tf_op jit(solution)/shard_map/all_to_all | solution.py:101
  45.7 35.8 %all-to-all-start = ((bf16[128,16,128]{0,2,1:T(8,128)(2,1)}), bf16[128,16,128]{0,2,1:T(8,128)(2,1)S(1)}, u32[]{:S(2)}, u32[]{:S(2)}) async-start(bf16[128,16,128]{0,2,1:T(8,128)(2,1)} %bitcast.2), calls=%async_computation | async-start | bytes 1048576 | tf_op jit(solution)/shard_map/all_to_all | solution.py:102
  81.5 35.6 %all-to-all-start.2 = ((bf16[128,16,128]{0,2,1:T(8,128)(2,1)}), bf16[128,16,128]{0,2,1:T(8,128)(2,1)S(1)}, u32[]{:S(2)}, u32[]{:S(2)}) async-start(bf16[128,16,128]{0,2,1:T(8,128)(2,1)} %bitcast.10), calls=%async_computation.2 | async-start | bytes 1048576 | tf_op jit(solution)/shard_map/all_to_all | solution.py:103
  139.4 36.1 %copy-start = (bf16[2048,320]{0,1:T(8,128)(2,1)S(1)}, bf16[2048,320]{0,1:T(8,128)(2,1)}, u32[]{:S(2)}) copy-start(bf16[2048,320]{0,1:T(8,128)(2,1)} %param.13) | copy-start | bytes 3932164
  182.8 913.6 %all-to-all-start.4 = ((bf16[16,2048,320]{1,2,0:T(8,128)(2,1)}), bf16[16,2048,320]{1,2,0:T(8,128)(2,1)}, u32[]{:S(2)}, u32[]{:S(2)}) async-start(bf16[16,2048,320]{1,2,0:T(8,128)(2,1)} %stack.2), calls=%async_computation.4 | async-start | bytes 41943040 | tf_op jit(solution)/shard_map/all_to_all | solution.py:14
  1107.8 6.1 copy-start.2
